TPU v7x, 32 devices: a whole 2x2x4 slice. The times are simulated.
32 devices in a mesh: groups: 2 (over x), row: 8 (over z, y), head: 2 (over core).
Axes of the slice: x: 2, y: 2, z: 4, core: 2. Of those that a mesh axis runs over, the one named last changes fastest.
Arguments:
- hidden: bfloat16 [48, 4096], P('groups'), parts along dimension 0, may hold values from -6 to 6
- norm_gain: float32 [4096], replicated, may hold values from 0.1 to 1.9
- w_query: bfloat16 [8, 256, 4096], P('head', 'row'), may hold values from -0.09375 to 0.09375
- w_key: bfloat16 [8, 256, 4096], P('head', 'row'), may hold values from -0.09375 to 0.09375
- w_value: bfloat16 [8, 512, 4096], P('head', 'row'), may hold values from -0.09375 to 0.09375
- w_outgate: bfloat16 [8, 512, 4096], P('head', 'row'), may hold values from -0.09375 to 0.09375
- w_out: bfloat16 [8, 512, 4096], P('head', 'row'), may hold values from -0.125 to 0.125
- w_gates: bfloat16 [2, 8, 4096], P(None, 'head'), may hold values from -0.09375 to 0.09375
- gate_bias: float32 [2, 8], P(None, 'head'), may hold values from -2 to 4
- headnorm_gain: float32 [8, 512], P('head', 'row'), may hold values from 0.1 to 1.9
- final_gain: float32 [4096], replicated, may hold values from 0.1 to 1.9
- w_vocab: bfloat16 [25152, 4096], P(('row', 'head')), may hold values from -39.0625 to 39.0625
- memory: float32 [48, 8, 256, 512], P('groups', 'head', 'row'), parts along dimension 0, may hold values from -6 to 6
- normalizer: float32 [48, 8, 256], P('groups', 'head', 'row'), parts along dimension 0, may hold values from -6 to 6
- stabilizer: float32 [48, 8], P('groups', 'head'), parts along dimension 0, may hold values from -2 to 2
- targets: int32 [48], P('groups'), parts along dimension 0, may hold values from 0 to 25151
Outputs:
- memory_out: float32 [48, 8, 256, 512], P('groups', 'head', 'row'), parts along dimension 0
- normalizer_out: float32 [48, 8, 256], P('groups', 'head', 'row'), parts along dimension 0
- stabilizer_out: float32 [48, 8], P('groups', 'head'), parts along dimension 0
- hidden_out: bfloat16 [48, 4096], P('groups', ('row', 'head')), parts along dimension 0
- log_prob: float32 [48], P('groups'), parts along dimension 0
There are 2 independent parts, one for each index of `groups`. A program takes and returns all parts, laid end to end along the dimension named above; an argument that names none is the same for every part. Nothing has to cross between parts.
All inputs are finite; a program needn't handle non-finite values.
Results may differ from a plain program's by a relative error of at most 0.0035.
The roundings to bfloat16 on the way count: a program that leaves them out, or rounds other values in their place, can miss the bound.
Values may be sent and summed in bfloat16 or wider, within the bound.
A program may use at most 64 MiB of HBM per device.

v0:
```python
import math
import jax
import jax.numpy as jnp
from jax import lax
from jax.sharding import PartitionSpec as P

QK_DIM = 256
epsilon = 1e-06


def joined_2(value, axis, join):
    pieces = jax.tree.map(lambda part: lax.all_gather(part, axis), value)
    head = jax.tree.map(lambda part: part[0], pieces)
    tail = jax.tree.map(lambda part: part[1:], pieces)
    total, _ = lax.scan(lambda total, share: (join(total, share), None), head, tail)
    return total


def rms_round(stream, gain):
    scale = lax.rsqrt(jnp.mean(stream * stream, axis=-1, keepdims=True) + epsilon)
    return (stream * scale * gain).astype(jnp.bfloat16)


def per_device(
    hidden,
    norm_gain,
    w_query,
    w_key,
    w_value,
    w_outgate,
    w_out,
    w_gates,
    gate_bias,
    headnorm_gain,
    final_gain,
    w_vocab,
    memory,
    normalizer,
    stabilizer,
    targets,
):
    value_rows = w_value.shape[1]
    stream = hidden.astype(jnp.float32)
    normed_in = rms_round(stream, norm_gain)

    def project(weights):
        return jnp.einsum("sd,hjd->shj", normed_in, weights, preferred_element_type=jnp.float32)

    queries = project(w_query) / math.sqrt(QK_DIM)
    key_part = project(w_key)
    value_part = project(w_value).astype(jnp.bfloat16)
    outgate_pre = project(w_outgate)
    gate_pre = (
        jnp.einsum("sd,ghd->gsh", normed_in, w_gates, preferred_element_type=jnp.float32)
        + gate_bias[:, None, :]
    )
    log_forget = jax.nn.log_sigmoid(gate_pre[1])
    stabilizer_out = jnp.maximum(log_forget + stabilizer, gate_pre[0])
    decay_rate = jnp.exp(log_forget + stabilizer - stabilizer_out)
    inflow = jnp.exp(gate_pre[0] - stabilizer_out)
    scaled_key = inflow[:, :, None] * key_part
    memory_out = (
        decay_rate[:, :, None, None] * memory
        + scaled_key[:, :, :, None]
        * lax.all_gather(value_part, "row", axis=2, tiled=True).astype(jnp.float32)[:, :, None, :]
    )
    normalizer_out = decay_rate[:, :, None] * normalizer + scaled_key
    partial_readout = jnp.einsum(
        "shj,shje->she", queries, memory_out, precision=lax.Precision.HIGHEST
    )
    readout = lax.psum(partial_readout, "row")
    average = jnp.mean(readout, axis=-1)
    centered_full = readout - average[:, :, None]
    variance = jnp.mean(centered_full * centered_full, axis=-1)
    centered = lax.dynamic_slice_in_dim(
        centered_full, lax.axis_index("row") * value_rows, value_rows, 2
    )
    normed = centered * lax.rsqrt(variance + epsilon)[:, :, None] * headnorm_gain
    gated_out = (jax.nn.sigmoid(outgate_pre) * normed).astype(jnp.bfloat16)
    partial_terms = jnp.einsum("shj,hjd->sd", gated_out, w_out, preferred_element_type=jnp.float32)
    position = lax.axis_index("row") * lax.axis_size("head") + lax.axis_index("head")
    share_width = hidden.shape[1] // (lax.axis_size("row") * lax.axis_size("head"))
    vocab_here = w_vocab.shape[0]
    projection = lax.psum(partial_terms, ("row", "head"))
    new_full = (stream + projection).astype(jnp.bfloat16)
    final_feat = rms_round(new_full.astype(jnp.float32), final_gain)
    logits = jnp.einsum("sd,vd->sv", final_feat, w_vocab, preferred_element_type=jnp.float32)
    hidden_out = lax.dynamic_slice_in_dim(new_full, position * share_width, share_width, 1)
    local_ids = targets - position * vocab_here
    is_target = jnp.arange(vocab_here, dtype=jnp.int32)[None, :] == local_ids[:, None]
    target_term = jnp.sum(jnp.where(is_target, logits, 0.0), axis=-1)
    local_max = jnp.max(logits, axis=-1)
    local_sum = jnp.sum(jnp.exp(logits - local_max[:, None]), axis=-1)

    def combine(earlier, later):
        highest = jnp.maximum(earlier[0], later[0])
        joined = earlier[1] * jnp.exp(earlier[0] - highest) + later[1] * jnp.exp(later[0] - highest)
        return (highest, joined, earlier[2] + later[2])

    highest, exp_total, picked = joined_2(
        (local_max, local_sum, target_term), ("row", "head"), combine
    )
    log_prob = picked - (highest + jnp.log(exp_total))
    return (memory_out, normalizer_out, stabilizer_out, hidden_out, log_prob)


def solution(mesh):
    in_specs = (
        P("groups", None),
        P(),
        P("head", "row", None),
        P("head", "row", None),
        P("head", "row", None),
        P("head", "row", None),
        P("head", "row", None),
        P(None, "head", None),
        P(None, "head"),
        P("head", "row"),
        P(),
        P(("row", "head"), None),
        P("groups", "head", "row", None),
        P("groups", "head", "row"),
        P("groups", "head"),
        P("groups"),
    )
    out_specs = (
        P("groups", "head", "row", None),
        P("groups", "head", "row"),
        P("groups", "head"),
        P("groups", ("row", "head")),
        P("groups"),
    )
    return jax.shard_map(
        per_device, mesh=mesh, in_specs=in_specs, out_specs=out_specs, check_vma=False
    )
```

profile of v0, /device:TPU:0, one launch (start us, length us, event | category | flops | bytes accessed | tf_op | source)
XLA Modules:
  0.0 280.0 jit_solution(1592682969917463788)
XLA Ops:
  7.2 0.0 copy-start
  7.2 0.0 all-reduce.7.cloned.1.call-start
  7.2 1.2 fusion.17
  8.5 2.7 convolution_convert_fusion
  11.1 0.1 copy.34
  11.3 33.0 %all_gather.21 = bf16[24,4,512]{0,1,2:T(4,128)(2,1)S(1)} all-gather(bf16[24,4,64]{0,1,2:T(4,128)(2,1)S(1)} %copy.34), channel_id=1, replica_groups=mesh['groups'=2,'row'=8,'head'=2] {'row'}, dimensions={2}, use_global_device_ids=true | all-gather | bytes 110592 | tf_op jit(solution)/shard_map/all_gather | solution.py:65
  44.3 0.3 copy.35
  44.6 0.1 copy.36
  44.7 1.2 fusion.13
  45.9 0.7 subtract_exponential_fusion.1
  46.6 0.0 copy-start.5
  46.6 0.1 copy.32
  46.7 2.2 fusion.28
  48.9 2.2 fusion.7
  51.1 3.4 %multiply_add_fusion = f32[24,4,32,512]{3,2,1,0:T(8,128)S(1)} fusion(f32[24,4,32,512]{3,2,1,0:T(8,128)} %param.30, f32[24,4,512]{2,1,0:T(4,128)S(1)} %copy.36, f32[24,4,32]{2,1,0:T(4,128)S(1)} %copy.33, f32[24,4]{1,0:T(8,128)S(1)} %copy.32), kind=kLoop, calls=%fused_computation.10 | loop fusion | flops 4718592 | bytes 12792192 | tf_op jit(solution)/shard_map/add | solution.py:63
  54.5 0.0 copy-start.1
  54.5 2.7 copy-done.1
  57.2 0.0 copy-start.7
  57.2 0.0 copy-start.4
  57.2 3.1 %fusion.26 = f32[24,4,1,512]{3,2,1,0:T(1,128)S(1)} fusion(f32[24,4,32,512]{3,2,1,0:T(8,128)S(1)} %multiply_add_fusion, f32[24,4,32,1]{2,0,1,3:T(8,128)S(1)} %fusion.7), kind=kOutput, calls=%fused_computation.46 | convolution fusion | flops 18874368 | bytes 6500352 | tf_op jit(solution)/shard_map/shj,shje->she/dot_general | solution.py:68
  60.4 0.7 copy.47
  61.1 0.0 all-reduce.7.cloned.1.call-update
  61.1 0.0 all-reduce.9.cloned.1.call-start
  61.2 0.6 copy.38
  61.8 0.6 dynamic-slice
  63.1 70.0 %all-reduce.7.cloned.1.call-done = f32[24,4,512]{2,0,1:T(8,128)} async-done(((f32[24,4,512]{2,0,1:T(8,128)}), f32[24,4,512]{2,0,1:T(8,128)}) %all-reduce.7.cloned.1.call-update) | async-done | bytes 196624 | tf_op jit(solution)/shard_map/psum | solution.py:71
  133.1 1.0 reduce_sum.55
  134.1 1.1 multiply_reduce_fusion
  135.3 3.8 %convolution_bitcast_fusion = f32[24,4096]{1,0:T(8,128)} fusion(bf16[4,64,4096]{2,1,0:T(8,128)(2,1)S(1)} %copy-done, bf16[4,64,4096]{2,1,0:T(8,128)(2,1)} %param.23, f32[24,4,512]{2,0,1:T(8,128)S(1)} %get-tuple-element.86, s32[]{:T(128)S(6)} %select_n.16, f32[4,64]{1,0:T(4,128)S(1)} %copy-done.6, f32[24,4]{0,1:T(4,128)S(1)} %add_rsqrt_fusion, ...), kind=kOutput, calls=%fused_computation.11 | convolution fusion | flops 101099520 | bytes 4854276 | tf_op jit(solution)/shard_map/shj,hjd->sd/dot_general | solution.py:80
  139.0 0.0 all-reduce.9.cloned.1.call-update
  139.1 90.6 %all-reduce.9.cloned.1.call-done = f32[24,4096]{1,0:T(8,128)} async-done(((f32[24,4096]{1,0:T(8,128)}), f32[24,4096]{1,0:T(8,128)}) %all-reduce.9.cloned.1.call-update) | async-done | bytes 393232 | tf_op jit(solution)/shard_map/psum | solution.py:84
  229.6 1.2 fusion.14
  230.8 0.0 copy-done.4
  230.8 8.3 %fusion.50 = (f32[24]{0:T(128)S(1)}, f32[24,1572]{1,0:T(8,128)S(1)}) fusion(bf16[1572,4096]{1,0:T(8,128)(2,1)} %param.29, bf16[24,4096]{1,0:T(8,128)(2,1)S(1)} %get-tuple-element.84, f32[4096]{0:T(1024)S(1)} %copy-done.4, f32[24]{0:T(128)S(1)} %add_rsqrt_fusion.1), kind=kOutput, calls=%fused_computation.74 | convolution fusion | flops 309498688 | bytes 13241920 | tf_op jit(solution)/shard_map/sd,vd->sv/dot_general | solution.py:87
  239.1 0.2 dynamic-update-slice
  239.3 0.2 select_reduce_fusion
  239.6 0.2 dynamic-update-slice.1
  239.8 0.2 dynamic-update-slice.2
  240.0 30.9 %all-reduce.3 = (f32[384]{0:T(512)S(1)}, f32[384]{0:T(512)S(1)}, f32[384]{0:T(512)S(1)}) all-reduce(f32[384]{0:T(512)S(1)} %dynamic-update-slice, f32[384]{0:T(512)S(1)} %dynamic-update-slice.1, f32[384]{0:T(512)S(1)} %dynamic-update-slice.2), channel_id=2, replica_groups=mesh['groups'=2,'row'=8,'head'=2] {'row','head'}, use_global_device_ids=true, to_apply=%add | all-reduce | flops 1152 | bytes 9216
  271.0 0.1 slice.36
  271.0 0.1 slice.37
  271.1 0.1 slice.38
  271.2 0.6 constant_dynamic-slice_fusion.3
  271.8 0.1 reshape.55
  271.9 0.1 reshape.56
  271.9 0.1 reshape.57
  272.0 0.6 while.14
  272.7 0.5 add_subtract_fusion
  (39 shorter events, 0.5 us)
Async XLA Ops:
  7.2 128.1 %copy-start = (bf16[4,64,4096]{2,1,0:T(8,128)(2,1)S(1)}, bf16[4,64,4096]{2,1,0:T(8,128)(2,1)}, u32[]{:S(2)}) copy-start(bf16[4,64,4096]{2,1,0:T(8,128)(2,1)} %param.24) | copy-start | bytes 6291460
  7.2 125.9 %all-reduce.7.cloned.1.call-start = ((), (), s32[]{:S(2)}) async-start(), calls=%async_computation | async-start | bytes 393216 | tf_op jit(solution)/shard_map/psum | solution.py:71
  46.6 7.9 %copy-start.5 = (f32[24,4]{0,1:T(4,128)}, f32[24,4]{0,1:T(4,128)S(1)}, u32[]{:S(2)}) copy-start(f32[24,4]{0,1:T(4,128)S(1)} %get-tuple-element.88) | copy-start | bytes 1156
  54.5 2.7 copy-start.1
  57.2 4.6 %copy-start.8 = (u32[32]{0:T(128)S(1)}, u32[32]{0:T(128)}, u32[]{:S(2)}) copy-start(u32[32]{0:T(128)} %constant.57) | copy-start | bytes 388
  57.2 78.0 %copy-start.2 = (bf16[24,4096]{1,0:T(8,128)(2,1)S(1)}, bf16[24,4096]{1,0:T(8,128)(2,1)}, u32[]{:S(2)}) copy-start(bf16[24,4096]{1,0:T(8,128)(2,1)} %param.18) | copy-start | bytes 589828
  57.2 78.0 %copy-start.3 = (f32[4096]{0:T(1024)S(1)}, f32[4096]{0:T(1024)}, u32[]{:S(2)}) copy-start(f32[4096]{0:T(1024)} %param.19) | copy-start | bytes 49156
  57.2 78.1 %copy-start.6 = (f32[4,64]{1,0:T(4,128)S(1)}, f32[4,64]{1,0:T(4,128)}, u32[]{:S(2)}) copy-start(f32[4,64]{1,0:T(4,128)} %param.27) | copy-start | bytes 3076
  57.2 81.8 %copy-start.7 = (s32[24]{0:T(128)S(1)}, s32[24]{0:T(128)}, u32[]{:S(2)}) copy-start(s32[24]{0:T(128)} %param.33) | copy-start | bytes 292
  57.2 173.6 %copy-start.4 = (f32[4096]{0:T(1024)S(1)}, f32[4096]{0:T(1024)}, u32[]{:S(2)}) copy-start(f32[4096]{0:T(1024)} %param.28) | copy-start | bytes 49156
  61.1 168.5 %all-reduce.9.cloned.1.call-start = ((), (), s32[]{:S(2)}) async-start(), calls=%async_computation.1 | async-start | bytes 786432 | tf_op jit(solution)/shard_map/psum | solution.py:84
Sparse Core Ops, SparseCore 0:
  61.2 71.7 all-reduce.6
  139.2 90.4 all-reduce.8
where the time goes:
time: 281 us; the launch traced here: 280 us
  waiting for transfers between devices  161 us (57%)
  blocking collectives  64 us (23%)
  matrix products  23.4 us (8%)
  between operations  15 us (5%)
  other arithmetic  9.78 us (3%)
  local copies, waits for them, and re-layouts  7.02 us (2%)
    psum x1, waiting for transfers between devices, per_device(): projection = lax.psum(partial_terms, ('row', 'head'))  90.6 us
    psum x1, waiting for transfers between devices, per_device(): readout = lax.psum(partial_readout, 'row')  70 us
    all_gather x1, blocking collectives, per_device(): lax.all_gather(value_part, 'row', axis=2, tiled=True).astype(jnp.float32)  33 us
    unnamed x1, blocking collectives  30.9 us
    dot_general x1, matrix products, per_device(): jnp.einsum('sd,vd->sv', final_feat, w_vocab, preferred_element_type=jnp.f...  8.26 us
    dot_general x3, matrix products, project(): jnp.einsum('sd,hjd->shj', normed_in, weights, preferred_element_type=jnp....  7.03 us
  transfers between devices with their start and end apart: 2, of which 2 were waited for; matrix products, arithmetic and copies ran while one was open for 0% of the time, Pallas kernels for 0%

commit v1 on v0

--- a/solution.py
+++ b/solution.py
@@ -39,6 +39,11 @@
     stabilizer,
     targets,
 ):
+
+    def _work_indices(work_x, group_axis):
+        step_out = jnp.sum(jax.lax.all_gather(work_x, group_axis), axis=0)
+        return step_out
+
     value_rows = w_value.shape[1]
     stream = hidden.astype(jnp.float32)
     normed_in = rms_round(stream, norm_gain)
@@ -68,7 +73,7 @@
     partial_readout = jnp.einsum(
         "shj,shje->she", queries, memory_out, precision=lax.Precision.HIGHEST
     )
-    readout = lax.psum(partial_readout, "row")
+    readout = _work_indices(partial_readout, group_axis="row")
     average = jnp.mean(readout, axis=-1)
     centered_full = readout - average[:, :, None]
     variance = jnp.mean(centered_full * centered_full, axis=-1)

time: 281 us -> 255 us (0.907)
  waiting for transfers between devices: 161 us -> 133 us
    psum x1 -> x0, waiting for transfers between devices: 70 us -> none  [per_device(): readout = lax.psum(partial_readout, 'row')]
    all_gather x0 -> x1, waiting for transfers between devices: none -> 43.5 us  [_work_indices(): step_out = jnp.sum(jax.lax.all_gather(work_x, group_axis), axis=0)]
where the time goes in v1:
time: 255 us; the launch traced here: 254 us
  waiting for transfers between devices  133 us (52%)
  blocking collectives  64 us (25%)
  matrix products  23.4 us (9%)
  between operations  15 us (6%)
  other arithmetic  11.3 us (4%)
  local copies, waits for them, and re-layouts  7.08 us (3%)
    psum x1, waiting for transfers between devices, per_device(): projection = lax.psum(partial_terms, ('row', 'head'))  89.9 us
    all_gather x1, waiting for transfers between devices, _work_indices(): step_out = jnp.sum(jax.lax.all_gather(work_x, group_axis), axis=0)  43.5 us
    all_gather x1, blocking collectives, per_device(): lax.all_gather(value_part, 'row', axis=2, tiled=True).astype(jnp.float32)  33 us
    unnamed x1, blocking collectives  30.9 us
    dot_general x1, matrix products, per_device(): jnp.einsum('sd,vd->sv', final_feat, w_vocab, preferred_element_type=jnp.f...  8.26 us
    dot_general x3, matrix products, project(): jnp.einsum('sd,hjd->shj', normed_in, weights, preferred_element_type=jnp....  7.03 us
  transfers between devices with their start and end apart: 2, of which 2 were waited for; matrix products, arithmetic and copies ran while one was open for 0% of the time, Pallas kernels for 0%

profile of v1, /device:TPU:0, one launch (start us, length us, event | category | flops | bytes accessed | tf_op | source)
XLA Modules:
  0.0 254.4 jit_solution(5920472809546466707)
XLA Ops:
  7.2 0.0 copy-start
  7.2 0.0 all-gather.6.cloned.1.call-start
  7.2 1.2 fusion.17
  8.5 2.7 %convolution_convert_fusion = bf16[24,4,64]{2,0,1:T(8,128)(2,1)S(1)} fusion(bf16[4,64,4096]{2,1,0:T(8,128)(2,1)} %param.22, bf16[24,4096]{1,0:T(8,128)(2,1)} %param.18, f32[4096]{0:T(1024)} %param.19, f32[24]{0:T(128)S(1)} %add_rsqrt_fusion.2), kind=kOutput, calls=%fused_computation.21 | convolution fusion | flops 50731008 | bytes 2322528 | tf_op jit(solution)/shard_map/sd,hjd->shj/dot_general | solution.py:52
  11.1 0.1 copy.56
  11.3 33.0 %all_gather.27 = bf16[24,4,512]{0,1,2:T(4,128)(2,1)S(1)} all-gather(bf16[24,4,64]{0,1,2:T(4,128)(2,1)S(1)} %copy.56), channel_id=1, replica_groups=mesh['groups'=2,'row'=8,'head'=2] {'row'}, dimensions={2}, use_global_device_ids=true | all-gather | bytes 110592 | tf_op jit(solution)/shard_map/all_gather | solution.py:70
  44.3 0.3 copy.57
  44.6 0.1 copy.58
  44.7 1.2 fusion.13
  45.9 0.7 subtract_exponential_fusion.1
  46.6 0.1 copy.54
  46.7 2.2 fusion.28
  48.9 2.2 fusion.7
  51.1 3.4 %multiply_add_fusion = f32[24,4,32,512]{3,2,1,0:T(8,128)S(1)} fusion(f32[24,4,32,512]{3,2,1,0:T(8,128)} %param.30, f32[24,4,512]{2,1,0:T(4,128)S(1)} %copy.58, f32[24,4,32]{2,1,0:T(4,128)S(1)} %copy.55, f32[24,4]{1,0:T(8,128)S(1)} %copy.54), kind=kLoop, calls=%fused_computation.10 | loop fusion | flops 4718592 | bytes 12792192 | tf_op jit(solution)/shard_map/add | solution.py:68
  54.5 0.0 copy-start.1
  54.5 2.7 %copy-done.1 = f32[24,4,32,512]{3,2,1,0:T(8,128)} copy-done((f32[24,4,32,512]{3,2,1,0:T(8,128)}, f32[24,4,32,512]{3,2,1,0:T(8,128)S(1)}, u32[]{:S(2)}) %copy-start.1) | copy-done | bytes 6291480
  57.2 3.1 %fusion.26 = f32[24,4,1,512]{3,2,1,0:T(1,128)S(1)} fusion(f32[24,4,32,512]{3,2,1,0:T(8,128)S(1)} %multiply_add_fusion, f32[24,4,32,1]{2,0,1,3:T(8,128)S(1)} %fusion.7), kind=kOutput, calls=%fused_computation.46 | convolution fusion | flops 18874368 | bytes 6500352 | tf_op jit(solution)/shard_map/shj,shje->she/dot_general | solution.py:73
  60.3 0.0 copy-start.7
  60.3 0.0 copy-start.4
  60.4 0.7 copy.74
  61.1 0.0 all-gather.6.cloned.1.call-update
  61.1 0.0 all-reduce.6.cloned.1.call-start
  61.2 0.6 copy.62
  61.8 0.6 dynamic-slice
  63.0 43.5 %all-gather.6.cloned.1.call-done = f32[192,4,512]{2,1,0:T(4,128)} async-done(((f32[24,4,512]{2,1,0:T(4,128)}), f32[192,4,512]{2,1,0:T(4,128)}) %all-gather.6.cloned.1.call-update) | async-done | bytes 1572880 | tf_op jit(solution)/shard_map/all_gather | solution.py:44
  106.6 1.7 reduce.1
  108.3 0.1 copy.65
  108.4 1.7 reduce_sum.64
  110.1 0.2 multiply_reduce_fusion
  110.3 3.8 %convolution_bitcast_fusion = f32[24,4096]{1,0:T(8,128)} fusion(bf16[4,64,4096]{2,1,0:T(8,128)(2,1)S(1)} %copy-done, bf16[4,64,4096]{2,1,0:T(8,128)(2,1)} %param.23, f32[24,4,512]{2,0,1:T(8,128)S(1)} %get-tuple-element.101, s32[]{:T(128)S(6)} %select_n.16, f32[4,64]{1,0:T(4,128)S(1)} %copy-done.6, f32[24,4]{0,1:T(4,128)S(1)} %add_rsqrt_fusion, ...), kind=kOutput, calls=%fused_computation.11 | convolution fusion | flops 101099520 | bytes 4854276 | tf_op jit(solution)/shard_map/shj,hjd->sd/dot_general | solution.py:85
  114.0 0.0 all-reduce.6.cloned.1.call-update
  114.1 89.9 %all-reduce.6.cloned.1.call-done = f32[24,4096]{1,0:T(8,128)} async-done(((f32[24,4096]{1,0:T(8,128)}), f32[24,4096]{1,0:T(8,128)}) %all-reduce.6.cloned.1.call-update) | async-done | bytes 393232 | tf_op jit(solution)/shard_map/psum | solution.py:89
  204.0 1.2 fusion.14
  205.1 8.3 %fusion.50 = (f32[24]{0:T(128)S(1)}, f32[24,1572]{1,0:T(8,128)S(1)}) fusion(bf16[1572,4096]{1,0:T(8,128)(2,1)} %param.29, bf16[24,4096]{1,0:T(8,128)(2,1)S(1)} %get-tuple-element.99, f32[4096]{0:T(1024)S(1)} %copy-done.4, f32[24]{0:T(128)S(1)} %add_rsqrt_fusion.1), kind=kOutput, calls=%fused_computation.74 | convolution fusion | flops 309498688 | bytes 13241920 | tf_op jit(solution)/shard_map/sd,vd->sv/dot_general | solution.py:92
  213.4 0.2 dynamic-update-slice
  213.7 0.2 select_reduce_fusion
  213.9 0.2 dynamic-update-slice.1
  214.1 0.2 dynamic-update-slice.2
  214.3 30.9 %all-reduce.3 = (f32[384]{0:T(512)S(1)}, f32[384]{0:T(512)S(1)}, f32[384]{0:T(512)S(1)}) all-reduce(f32[384]{0:T(512)S(1)} %dynamic-update-slice, f32[384]{0:T(512)S(1)} %dynamic-update-slice.1, f32[384]{0:T(512)S(1)} %dynamic-update-slice.2), channel_id=3, replica_groups=mesh['groups'=2,'row'=8,'head'=2] {'row','head'}, use_global_device_ids=true, to_apply=%add | all-reduce | flops 1152 | bytes 9216
  245.3 0.1 slice.36
  245.4 0.1 slice.37
  245.4 0.1 slice.38
  245.5 0.6 constant_dynamic-slice_fusion.3
  246.1 0.1 reshape.57
  246.2 0.1 reshape.58
  246.3 0.1 reshape.59
  246.4 0.6 while.14
  247.0 0.5 add_subtract_fusion
  (42 shorter events, 0.5 us)
Async XLA Ops:
  7.2 103.1 %copy-start = (bf16[4,64,4096]{2,1,0:T(8,128)(2,1)S(1)}, bf16[4,64,4096]{2,1,0:T(8,128)(2,1)}, u32[]{:S(2)}) copy-start(bf16[4,64,4096]{2,1,0:T(8,128)(2,1)} %param.24) | copy-start | bytes 6291460
  7.2 99.4 %all-gather.6.cloned.1.call-start = ((), (), s32[]{:S(2)}) async-start(), calls=%async_computation.1 | async-start | bytes 1769472 | tf_op jit(solution)/shard_map/all_gather | solution.py:44
  46.6 7.9 %copy-start.5 = (f32[24,4]{0,1:T(4,128)}, f32[24,4]{0,1:T(4,128)S(1)}, u32[]{:S(2)}) copy-start(f32[24,4]{0,1:T(4,128)S(1)} %get-tuple-element.103) | copy-start | bytes 1156
  54.5 2.7 %copy-start.1 = (f32[24,4,32,512]{3,2,1,0:T(8,128)}, f32[24,4,32,512]{3,2,1,0:T(8,128)S(1)}, u32[]{:S(2)}) copy-start(f32[24,4,32,512]{3,2,1,0:T(8,128)S(1)} %multiply_add_fusion) | copy-start | bytes 18874372
  57.2 4.6 %copy-start.8 = (u32[32]{0:T(128)S(1)}, u32[32]{0:T(128)}, u32[]{:S(2)}) copy-start(u32[32]{0:T(128)} %constant.57) | copy-start | bytes 388
  57.2 53.1 %copy-start.2 = (bf16[24,4096]{1,0:T(8,128)(2,1)S(1)}, bf16[24,4096]{1,0:T(8,128)(2,1)}, u32[]{:S(2)}) copy-start(bf16[24,4096]{1,0:T(8,128)(2,1)} %param.18) | copy-start | bytes 589828
  57.2 53.1 %copy-start.3 = (f32[4096]{0:T(1024)S(1)}, f32[4096]{0:T(1024)}, u32[]{:S(2)}) copy-start(f32[4096]{0:T(1024)} %param.19) | copy-start | bytes 49156
  57.2 53.1 %copy-start.6 = (f32[4,64]{1,0:T(4,128)S(1)}, f32[4,64]{1,0:T(4,128)}, u32[]{:S(2)}) copy-start(f32[4,64]{1,0:T(4,128)} %param.27) | copy-start | bytes 3076
  60.3 53.7 %copy-start.7 = (s32[24]{0:T(128)S(1)}, s32[24]{0:T(128)}, u32[]{:S(2)}) copy-start(s32[24]{0:T(128)} %param.33) | copy-start | bytes 292
  60.3 144.8 %copy-start.4 = (f32[4096]{0:T(1024)S(1)}, f32[4096]{0:T(1024)}, u32[]{:S(2)}) copy-start(f32[4096]{0:T(1024)} %param.28) | copy-start | bytes 49156
  61.1 142.9 %all-reduce.6.cloned.1.call-start = ((), (), s32[]{:S(2)}) async-start(), calls=%async_computation | async-start | bytes 786432 | tf_op jit(solution)/shard_map/psum | solution.py:89
Sparse Core Ops, SparseCore 0:
  61.2 45.2 all-gather.5
  114.2 89.7 all-reduce.5
